TPU v7x, 256 devices: a whole 4x4x8 slice. The times are simulated.
256 devices in a mesh: dp: 64 (over z, x_hi, y), mp: 4 (over x_lo, core).
Axes of the slice: x: 4 (x_hi: 2, x_lo: 2; x = x_hi * 2 + x_lo), y: 4, z: 8, core: 2. Of those that a mesh axis runs over, the one named last changes fastest.
Arguments:
- gradients: bfloat16 [64, 1024, 6144], P('dp', None, 'mp'), may hold values from -128 to 128
- weights: bfloat16 [1024, 6144], P(None, 'mp'), may hold values from -3 to 3
- master: float32 [1024, 6144], P('dp', 'mp'), may hold values from -6 to 6
- moment_one: float32 [1024, 6144], P('dp', 'mp'), may hold values from -6 to 6
- moment_two: float32 [1024, 6144], P('dp', 'mp'), may hold values from 0.25 to 4
- group_ids: int32 [1024], replicated, may hold values from 0 to 31, never falling along the last dimension, each value on 1 to 64 neighbouring positions
Outputs:
- new_weights: bfloat16 [1024, 6144], P(None, 'mp')
- new_master: float32 [1024, 6144], P('dp', 'mp')
- new_first: float32 [1024, 6144], P('dp', 'mp')
- new_second: float32 [1024, 6144], P('dp', 'mp')
Inputs may be any that keep to these rules, and one draw needn't show every extreme that they name: `group_ids`: group numbers never fall along the rows; each group has 1 to 64 rows and every group is present.
All inputs are finite; a program needn't handle non-finite values.
Results may differ from a plain program's by a relative error of at most 0.001.
The roundings to bfloat16 on the way count: a program that leaves them out, or rounds other values in their place, can miss the bound.
Values may be sent and summed in bfloat16 or wider, within the bound.
A program may use at most 64 MiB of HBM per device.

v0:
```python
import functools

import jax
import jax.numpy as jnp
from jax import lax
from jax.sharding import Mesh
from jax.sharding import PartitionSpec as P

DP = ("dp_0", "dp_1", "dp_2")
DP_MP = ("dp_0", "dp_1", "dp_2", "mp_0", "mp_1")
MP = ("mp_0", "mp_1")


beta_one = 0.9
beta_two = 0.999
adam_eps = 1e-06
weight_decay = 0.01
learn_rate = 0.04
step_count = 100


def split_up(x, dim, count):
    before, after = (x.shape[:dim], x.shape[dim + 1 :])
    return jnp.moveaxis(x.reshape(*before, count, -1, *after), dim, 0)


def summed_on_arrival(x, axis, dim):
    parts = split_up(x, dim, lax.axis_size(axis))
    arrived = lax.all_to_all(parts, axis, split_axis=0, concat_axis=0, tiled=True)
    return arrived.astype(jnp.float32).sum(axis=0)


def by_axis(x, axes):
    return functools.reduce(lax.psum, axes, x)


def joined_along(parts, dim):
    dims = list(parts.shape[1:])
    dims[dim] *= parts.shape[0]
    return jnp.moveaxis(parts, 0, dim).reshape(dims)


def gather_in_order(x, axes, sequence):
    parts = x[None]
    for k in sequence:
        parts = lax.all_gather(parts, axes[k], axis=0, tiled=True)
    current = [lax.axis_size(axes[k]) for k in reversed(sequence)]
    parts = parts.reshape(*current, *x.shape)
    turned = sorted(range(len(sequence)), key=lambda place: sequence[len(sequence) - 1 - place])
    return parts.transpose(*turned, *range(len(sequence), parts.ndim)).reshape(-1, *x.shape)


def whole_of(x, axes, sequence, dim):
    return joined_along(gather_in_order(x, axes, sequence), dim)


def on_device(gradients, weights, master, moment_one, moment_two, group_ids):
    owned_rows = master.shape[0]
    rows_all = weights.shape[0]
    groups = rows_all // 32
    replicas = lax.axis_size(DP)
    my_index = lax.axis_index(DP)
    first_own = my_index * owned_rows
    my_groups = lax.dynamic_slice_in_dim(group_ids, first_own, owned_rows, 0)
    member = (my_groups[:, None] == jnp.arange(groups, dtype=jnp.int32)[None, :]).astype(
        jnp.float32
    )
    weight_rows = jnp.dot(jnp.sum(master * master, axis=1), member, precision=lax.Precision.HIGHEST)
    local_grad = gradients[0]
    summed = summed_on_arrival(local_grad.astype(jnp.float32).astype(jnp.bfloat16), DP, 0)
    grad_mean = summed / replicas
    new_first = beta_one * moment_one + (1.0 - beta_one) * grad_mean
    new_second = beta_two * moment_two + (1.0 - beta_two) * grad_mean * grad_mean
    correct_one = 1.0 - beta_one**step_count
    correct_two = 1.0 - beta_two**step_count
    update = (
        new_first / correct_one / (jnp.sqrt(new_second / correct_two) + adam_eps)
        + weight_decay * master
    )
    update_rows = jnp.dot(jnp.sum(update * update, axis=1), member, precision=lax.Precision.HIGHEST)
    weight_sq, update_sq = (by_axis(weight_rows, DP_MP), by_axis(update_rows, DP_MP))
    trust_ratio = jnp.sqrt(weight_sq / (update_sq + 1e-06))
    row_ratio = jnp.dot(member, trust_ratio, precision=lax.Precision.HIGHEST)
    step_size = learn_rate * row_ratio[:, None] * update
    new_master = master - step_size
    delta_bf = (-step_size).astype(jnp.bfloat16)
    new_weights = (
        weights.astype(jnp.float32) + whole_of(delta_bf, DP, (1, 0, 2), 0).astype(jnp.float32)
    ).astype(jnp.bfloat16)
    return (new_weights, new_master, new_first, new_second)


def solution(mesh):
    torus = Mesh(mesh.devices.reshape(8, 2, 4, 2, 2), ("dp_0", "dp_1", "dp_2", "mp_0", "mp_1"))
    placed = (P(DP, None, MP), P(None, MP), P(DP, MP), P(DP, MP), P(DP, MP), P())
    return jax.shard_map(
        on_device,
        mesh=torus,
        in_specs=placed,
        out_specs=(P(None, MP), P(DP, MP), P(DP, MP), P(DP, MP)),
        check_vma=False,
    )
```

profile of v0, /device:TPU:16, one launch (start us, length us, event | category | flops | bytes accessed | tf_op | source)
XLA Modules:
  0.0 221.6 jit_solution(12461575750495941655)
XLA Ops:
  7.2 14.5 %all-to-all-start = ((bf16[64,16,1536]{2,1,0:T(8,128)(2,1)}), bf16[64,16,1536]{2,1,0:T(8,128)(2,1)S(1)}, u32[]{:S(2)}, u32[]{:S(2)}) async-start(bf16[64,16,1536]{2,1,0:T(8,128)(2,1)} %bitcast.27), calls=%async_computation | async-start | bytes 6291456 | tf_op jit(solution)/shard_map/all_to_all | solution.py:29
  21.6 0.0 copy-start.1
  21.6 0.0 copy-start.2
  21.7 0.0 copy-start.3
  21.7 0.0 all-gather.3.cloned.1.call-start
  21.7 0.8 dynamic_slice.3
  22.5 72.0 %all-to-all-done = bf16[64,16,1536]{2,1,0:T(8,128)(2,1)S(1)} async-done(((bf16[64,16,1536]{2,1,0:T(8,128)(2,1)}), bf16[64,16,1536]{2,1,0:T(8,128)(2,1)S(1)}, u32[]{:S(2)}, u32[]{:S(2)}) %all-to-all-start) | async-done | bytes 3145760 | tf_op jit(solution)/shard_map/all_to_all | solution.py:29
  94.5 0.5 convert_reduce_fusion
  94.9 0.0 copy-done.1
  94.9 0.0 copy-done.2
  95.0 0.0 copy-done.3
  95.0 0.9 multiply_reduce_fusion
  95.8 0.2 convolution_bitcast_fusion.1
  96.0 0.2 convolution_bitcast_fusion.2
  96.2 15.6 %all-reduce = (f32[32]{0:T(128)S(1)}, f32[32]{0:T(128)S(1)}) all-reduce(f32[32]{0:T(128)S(1)} %convolution_bitcast_fusion.2, f32[32]{0:T(128)S(1)} %convolution_bitcast_fusion.1), channel_id=1, replica_groups=mesh['dp_0'=8,'dp_1'=2,'dp_2'=4,'mp_0'=2,'mp_1'=2] {'dp_0'}, use_global_device_ids=true, to_apply=%region_1.0 | all-reduce | flops 64 | bytes 512 | tf_op jit(solution)/shard_map/psum | solution.py:34
  111.8 6.4 %all-reduce.4 = (f32[32]{0:T(128)S(1)}, f32[32]{0:T(128)S(1)}) all-reduce(f32[32]{0:T(128)S(1)} %get-tuple-element.4, f32[32]{0:T(128)S(1)} %get-tuple-element.5), channel_id=1, replica_groups=mesh['dp_0'=8,'dp_1'=2,'dp_2'=4,'mp_0'=2,'mp_1'=2] {'dp_1'}, use_global_device_ids=true, to_apply=%region_2.0 | all-reduce | flops 64 | bytes 512 | tf_op jit(solution)/shard_map/psum | solution.py:34
  118.2 7.5 %all-reduce.1 = (f32[32]{0:T(128)S(1)}, f32[32]{0:T(128)S(1)}) all-reduce(f32[32]{0:T(128)S(1)} %get-tuple-element.12, f32[32]{0:T(128)S(1)} %get-tuple-element.13), channel_id=1, replica_groups=mesh['dp_0'=8,'dp_1'=2,'dp_2'=4,'mp_0'=2,'mp_1'=2] {'dp_2'}, use_global_device_ids=true, to_apply=%region_3.0 | all-reduce | flops 64 | bytes 512 | tf_op jit(solution)/shard_map/psum | solution.py:34
  125.7 4.9 %all-reduce.3 = (f32[32]{0:T(128)S(1)}, f32[32]{0:T(128)S(1)}) all-reduce(f32[32]{0:T(128)S(1)} %get-tuple-element.6, f32[32]{0:T(128)S(1)} %get-tuple-element.7), channel_id=1, replica_groups=mesh['dp_0'=8,'dp_1'=2,'dp_2'=4,'mp_0'=2,'mp_1'=2] {'mp_0'}, use_global_device_ids=true, to_apply=%region_4.0 | all-reduce | flops 64 | bytes 512 | tf_op jit(solution)/shard_map/psum | solution.py:34
  130.6 2.4 %all-reduce.2 = (f32[32]{0:T(128)S(1)}, f32[32]{0:T(128)S(1)}) all-reduce(f32[32]{0:T(128)S(1)} %get-tuple-element.10, f32[32]{0:T(128)S(1)} %get-tuple-element.11), channel_id=1, replica_groups=mesh['dp_0'=8,'dp_1'=2,'dp_2'=4,'mp_0'=2,'mp_1'=2] {'mp_1'}, use_global_device_ids=true, to_apply=%region_5.0 | all-reduce | flops 64 | bytes 512 | tf_op jit(solution)/shard_map/psum | solution.py:34
  133.0 0.2 fusion.1
  133.2 0.7 multiply_subtract_fusion
  134.0 6.2 %all-gather = bf16[32,1536]{1,0:T(8,128)(2,1)S(1)} all-gather(bf16[16,1536]{1,0:T(8,128)(2,1)S(1)} %get-tuple-element.19), channel_id=2, replica_groups=mesh['dp_0'=8,'dp_1'=2,'dp_2'=4,'mp_0'=2,'mp_1'=2] {'dp_1'}, dimensions={0}, use_global_device_ids=true | all-gather | bytes 147456 | tf_op jit(solution)/shard_map/all_gather | solution.py:46
  140.2 28.1 %all_gather.10 = bf16[16,16,1536]{2,1,0:T(8,128)(2,1)} all-gather(bf16[2,16,1536]{2,1,0:T(8,128)(2,1)S(1)} %bitcast.29), channel_id=1, replica_groups=mesh['dp_0'=8,'dp_1'=2,'dp_2'=4,'mp_0'=2,'mp_1'=2] {'dp_0'}, dimensions={0}, use_global_device_ids=true | all-gather | bytes 884736 | tf_op jit(solution)/shard_map/all_gather | solution.py:46
  168.3 0.0 all-gather.3.cloned.1.call-update
  168.3 39.2 %all-gather.3.cloned.1.call-done = bf16[64,16,1536]{2,1,0:T(8,128)(2,1)} async-done(((bf16[16,16,1536]{2,1,0:T(8,128)(2,1)}), bf16[64,16,1536]{2,1,0:T(8,128)(2,1)}) %all-gather.3.cloned.1.call-update) | async-done | bytes 3145744 | tf_op jit(solution)/shard_map/all_gather | solution.py:46
  207.5 2.8 %convert_bitcast_fusion = f32[8,2,4,16,1536]{4,3,1,0,2:T(8,128)S(1)} fusion(bf16[4,8,2,16,1536]{4,3,2,1,0:T(8,128)(2,1)} %bitcast.28), kind=kLoop, calls=%fused_computation | loop fusion | flops 1572864 | bytes 9437184 | tf_op jit(solution)/shard_map/convert_element_type | solution.py:88
  210.2 0.0 copy-start
  210.3 0.4 copy.11
  210.7 1.4 copy-done
  212.1 2.7 %fusion = bf16[1024,1536]{1,0:T(8,128)(2,1)} fusion(f32[8,2,4,16,1536]{4,3,2,1,0:T(8,128)S(1)} %copy.11, bf16[1024,1536]{1,0:T(8,128)(2,1)S(1)} %copy-done), kind=kLoop, calls=%fused_computation.2 | loop fusion | flops 4718592 | bytes 12582912 | tf_op jit(solution)/shard_map/convert_element_type | solution.py:89
Async XLA Ops:
  7.2 87.3 %all-to-all-start = ((bf16[64,16,1536]{2,1,0:T(8,128)(2,1)}), bf16[64,16,1536]{2,1,0:T(8,128)(2,1)S(1)}, u32[]{:S(2)}, u32[]{:S(2)}) async-start(bf16[64,16,1536]{2,1,0:T(8,128)(2,1)} %bitcast.27), calls=%async_computation | async-start | bytes 6291456 | tf_op jit(solution)/shard_map/all_to_all | solution.py:29
  21.6 73.3 %copy-start.1 = (f32[16,1536]{1,0:T(8,128)S(1)}, f32[16,1536]{1,0:T(8,128)}, u32[]{:S(2)}) copy-start(f32[16,1536]{1,0:T(8,128)} %param.8) | copy-start | bytes 294916
  21.6 73.3 %copy-start.2 = (f32[16,1536]{1,0:T(8,128)S(1)}, f32[16,1536]{1,0:T(8,128)}, u32[]{:S(2)}) copy-start(f32[16,1536]{1,0:T(8,128)} %param.9) | copy-start | bytes 294916
  21.7 73.3 %copy-start.3 = (f32[16,1536]{1,0:T(8,128)S(1)}, f32[16,1536]{1,0:T(8,128)}, u32[]{:S(2)}) copy-start(f32[16,1536]{1,0:T(8,128)} %param.10) | copy-start | bytes 294916
  21.7 185.8 %all-gather.3.cloned.1.call-start = ((), (), s32[]{:S(2)}) async-start(), calls=%async_computation.1 | async-start | bytes 3932160 | tf_op jit(solution)/shard_map/all_gather | solution.py:46
  210.2 1.9 copy-start
Sparse Core Ops, SparseCore 0:
  168.4 39.0 all-gather.2
where the time goes:
time: 224 us; the launch traced here: 222 us
  waiting for transfers between devices  111 us (50%)
  blocking collectives  71.1 us (32%)
  starting transfers between devices  14.5 us (6%)
  between operations  14.1 us (6%)
  other arithmetic  7.49 us (3%)
  local copies, waits for them, and re-layouts  2.71 us (1%)
    all_to_all x1, waiting for transfers between devices, summed_on_arrival(): lax.all_to_all(parts, axis, split_axis=0, concat_axis=0, tiled=True)  72 us
    all_gather x1, waiting for transfers between devices, gather_in_order(): parts = lax.all_gather(parts, axes[k], axis=0, tiled=True)  39.2 us
    psum x5, blocking collectives, by_axis(): return functools.reduce(lax.psum, axes, x)  36.8 us
    all_gather x2, blocking collectives, gather_in_order(): parts = lax.all_gather(parts, axes[k], axis=0, tiled=True)  34.3 us
    all_to_all x1, starting transfers between devices, summed_on_arrival(): lax.all_to_all(parts, axis, split_axis=0, concat_axis=0, tiled=True)  14.5 us
  transfers between devices with their start and end apart: 2, of which 2 were waited for; matrix products, arithmetic and copies ran while one was open for 0% of the time, Pallas kernels for 0%

commit v1 on v0

v1 whole, which is shorter than its diff:
```python
import functools

import jax
import jax.numpy as jnp
from jax import lax
from jax.experimental import pallas as pl
from jax.experimental.pallas import tpu as pltpu
from jax.sharding import Mesh
from jax.sharding import PartitionSpec as P

MESH = pl.DeviceIdType.MESH
NAMES = ("z", "xh", "y", "xl", "c")
NZ, NX, NY = 8, 2, 4
ROWS, COLS = 16, 1536
CA = 1024
CB = COLS - CA
PA = 896
PC = COLS - PA
AHEAD = 2
N_SEM = 200

beta_one = 0.9
beta_two = 0.999
adam_eps = 1e-06
weight_decay = 0.01
learn_rate = 0.04
step_count = 100
correct_one = 1.0 - beta_one**step_count
correct_two = 1.0 - beta_two**step_count

f32, bf16 = jnp.float32, jnp.bfloat16


def kernel(
    g_hbm, w_ref, ma_ref, m1_ref, m2_ref, ids_ref,
    nw_ref, nm_ref, nf_ref, ns_ref,
    g, d, ra1, ra3, ra2, rl1, rl3, xs, xr, yp, zs, zr,
    b4, bf4, b3, bs2, br2, bs1, br1, bt, by2, bys, byr, bf, bxr,
    gs, ns1, nr1, ns2, nr2, load_sem, send_sem, recv_sem,
):
    z, x, y = lax.axis_index("z"), lax.axis_index("xh"), lax.axis_index("y")
    xl, core = lax.axis_index("xl"), lax.axis_index("c")
    ox = 1 - x

    def zo(k):
        return lax.rem(z + (k + NZ), NZ)

    def yo(k):
        return lax.rem(y + (k + NY), NY)

    me = (z * NX + x) * NY + y

    def owner(k):
        o = lax.rem(me + (k + 64), 64)
        return {"z": lax.div(o, 8), "xh": lax.rem(lax.div(o, 4), 2), "y": lax.rem(o, 4)}

    yu, yd, y2 = {"y": yo(1)}, {"y": yo(-1)}, {"y": yo(2)}
    zu, zd = {"z": zo(1)}, {"z": zo(-1)}
    xp = {"xh": ox}
    mp_peers = [{"c": 1 - core}, {"xl": 1 - xl}, {"xl": 1 - xl, "c": 1 - core}]
    dp_peers = [owner(k) for k in (1, -1, 2, -2, 3, -3, 4, -4)]

    order = [4, 3, -3, 2, -2, 1, -1, 0]
    loads = []
    for k, dz in enumerate(order):
        c = pltpu.make_async_copy(g_hbm.at[zo(dz)], g.at[zo(dz)], load_sem.at[k])
        c.start()
        loads.append(c)

    barrier = pltpu.get_barrier_semaphore()
    peers = [yu, yd, y2, zu, zd, xp] + mp_peers + dp_peers
    for p in peers:
        pl.semaphore_signal(barrier, 1, device_id=p, device_id_type=MESH)
    pl.semaphore_wait(barrier, len(peers))

    sent = []

    def send(src, dst, dev):
        i = len(sent)
        c = pltpu.make_async_remote_copy(
            src, dst, send_sem.at[i], recv_sem.at[i], device_id=dev, device_id_type=MESH
        )
        c.start()
        sent.append(c)
        return c

    a_cols = pl.ds(0, CA)
    b_cols = pl.ds(CA, CB)

    relay_up, relay_down, direct_up, direct_down, forward = {}, {}, {}, {}, {}
    cross, zup, zdown = {}, {}, {}

    def y_send(k):
        zz = zo(order[k])
        relay_up[k] = send(g.at[zz, 0, yo(2), :, a_cols], rl1.at[k], yu)
        relay_down[k] = send(g.at[zz, 1, yo(2), :, a_cols], rl3.at[k], yd)
        direct_up[k] = send(g.at[zz, :, yo(1), :, a_cols], ra1.at[k], yu)
        direct_down[k] = send(g.at[zz, :, yo(-1), :, a_cols], ra3.at[k], yd)

    def y_forward(k):
        relay_up[k].wait_recv()
        up = send(rl1.at[k], ra2.at[k, 0], yu)
        relay_down[k].wait_recv()
        forward[k] = (up, send(rl3.at[k], ra2.at[k, 1], yd))

    def y_sum(k):
        direct_up[k].wait_recv()
        direct_down[k].wait_recv()
        for c in forward[k]:
            c.wait_recv()
        zz = zo(order[k])

        def total(h):
            return (
                (g[zz, h, y, :, 0:CA].astype(f32) + ra1[k, h].astype(f32))
                + (ra3[k, h].astype(f32) + ra2[k, h].astype(f32))
            )

        xs[k] = total(ox)
        cross[k] = send(xs.at[k], xr.at[k], xp)
        yp[k] = total(x)

    def z_step(k):
        dz = order[k]
        cross[k].wait_recv()
        part = yp[k] + xr[k]
        if dz == 4:
            zs[k] = part
            zup[4] = send(zs.at[k, pl.ds(0, 8)], zr.at[k, pl.ds(0, 8)], zu)
            zdown[4] = send(zs.at[k, pl.ds(8, 8)], zr.at[k, pl.ds(8, 8)], zd)
            return
        if dz == 0:
            zup[1].wait_recv()
            zdown[1].wait_recv()
            gs[:, 0:CA] = part + (zr[order.index(1)] + zr[order.index(-1)])
            return
        chain, dev, far = (zup, zu, 1) if dz > 0 else (zdown, zd, -1)
        step = abs(dz)
        chain[step + 1].wait_recv()
        if step == 3:
            rows = slice(0, 8) if dz > 0 else slice(8, 16)
            rest = slice(8, 16) if dz > 0 else slice(0, 8)
            zs[k, rows] = part[rows] + zr[0, rows]
            zs[k, rest] = part[rest]
        else:
            zs[k] = part + zr[order.index(far * (step + 1))]
        chain[step] = send(zs.at[k], zr.at[k], dev)

    zdir = (zu, zd)
    sign = (1, -1)
    b4c, b3c, bfc, b2c, b1c = {}, {}, {}, {}, {}

    def own_b(dz, h):
        return g[zo(dz), h, :, :, CA:COLS].astype(f32)

    def b_raw4():
        for s in (0, 1):
            b4c[s] = send(g.at[zo(4), s, :, :, b_cols], b4.at[s], zdir[s])

    def b_raw3():
        for h_first in (1, 0):
            for s in (0, 1):
                h = h_first if s == 0 else 1 - h_first
                b3c[s, h] = send(g.at[zo(3 * sign[s]), h, :, :, b_cols], b3.at[s, h], zdir[s])

    def b_forward():
        for s in (0, 1):
            b4c[s].wait_recv()
            bfc[s] = send(b4.at[s], bf4.at[s], zdir[s])

    def b_two(first):
        for s in (0, 1):
            h = (1 - s) if first else s
            b3c[s, h].wait_recv()
            v = own_b(2 * sign[s], h) + b3[s, h].astype(f32)
            if not first:
                bfc[s].wait_recv()
                v = v + bf4[s].astype(f32)
            bs2[s, h] = v
            b2c[s, h] = send(bs2.at[s, h], br2.at[s, h], zdir[s])

    def b_one(first):
        for s in (0, 1):
            h = (1 - s) if first else s
            b2c[s, h].wait_recv()
            bs1[s, h] = own_b(sign[s], h) + br2[s, h]
            b1c[s, h] = send(bs1.at[s, h], br1.at[s, h], zdir[s])

    yc = {}

    def b_total():
        for s in (0, 1):
            for h in (0, 1):
                b1c[s, h].wait_recv()
        for h in (0, 1):
            bt[h] = own_b(0, h) + (br1[0, h] + br1[1, h])
        yc["two_up"] = send(bt.at[0, yo(2)], by2.at[0], yu)
        yc["two_down"] = send(bt.at[1, yo(2)], by2.at[1], yd)

    def b_y_one():
        yc["two_up"].wait_recv()
        bys[0, 0] = bt[0, yo(1)] + by2[0]
        bys[0, 1] = bt[1, yo(1)]
        yc["up"] = send(bys.at[0], byr.at[0], yu)
        yc["two_down"].wait_recv()
        bys[1, 0] = bt[0, yo(-1)]
        bys[1, 1] = bt[1, yo(-1)] + by2[1]
        yc["down"] = send(bys.at[1], byr.at[1], yd)

    def b_y_sum():
        yc["up"].wait_recv()
        yc["down"].wait_recv()
        bf[1] = bt[ox, y] + (byr[0, ox] + byr[1, ox])
        yc["x"] = send(bf.at[1], bxr, xp)
        bf[0] = bt[x, y] + (byr[0, x] + byr[1, x])

    def b_final():
        yc["x"].wait_recv()
        gs[:, CA:COLS] = bf[0] + bxr[...]

    slots = {
        1: [b_forward],
        2: [functools.partial(b_two, True)],
        3: [functools.partial(b_two, False)],
        4: [functools.partial(b_one, True)],
        5: [functools.partial(b_one, False)],
        7: [b_total],
        8: [b_y_one],
        9: [b_y_sum],
        10: [b_final],
    }

    loads[0].wait()
    b_raw4()
    y_send(0)
    loads[1].wait()
    loads[2].wait()
    b_raw3()
    y_send(1)
    for k in range(11):
        if 2 <= k + AHEAD < 8:
            if k + AHEAD > 2:
                loads[k + AHEAD].wait()
            y_send(k + AHEAD)
        if k < 8:
            y_forward(k)
        for f in slots.get(k, []):
            f()
        if 0 <= k - 1 < 8:
            y_sum(k - 1)
        if 0 <= k - 2 < 8:
            z_step(k - 2)

    row = lax.broadcasted_iota(jnp.int32, (ROWS, 128), 0)
    lane = lax.broadcasted_iota(jnp.int32, (ROWS, 128), 1)
    ids = jnp.zeros((ROWS, 128), jnp.int32)
    for i in range(ROWS):
        ids = jnp.where(row == i, ids_ref[me * ROWS + i], ids)
    member = (ids == lane).astype(f32)
    master = ma_ref[...]
    mean = gs[...] / 64.0
    new_first = beta_one * m1_ref[...] + (1.0 - beta_one) * mean
    new_second = beta_two * m2_ref[...] + (1.0 - beta_two) * mean * mean
    nf_ref[...] = new_first
    ns_ref[...] = new_second
    update = (
        new_first / correct_one / (jnp.sqrt(new_second / correct_two) + adam_eps)
        + weight_decay * master
    )
    gs[...] = update
    weight_rows = jnp.sum(master * master, axis=1, keepdims=True)
    update_rows = jnp.sum(update * update, axis=1, keepdims=True)
    weight_part = jnp.sum(member * weight_rows, axis=0, keepdims=True)
    update_part = jnp.sum(member * update_rows, axis=0, keepdims=True)
    first = lax.broadcasted_iota(jnp.int32, (8, 128), 0) == 0
    ns1[...] = jnp.where(first, weight_part, update_part)
    c1 = [send(ns1, nr1.at[i], p) for i, p in enumerate(mp_peers)]
    for c in c1:
        c.wait_recv()
    ns2[...] = (ns1[...] + nr1[0]) + (nr1[1] + nr1[2])
    c2 = [send(ns2, nr2.at[i], p) for i, p in enumerate(dp_peers)]
    for c in c2:
        c.wait_recv()
    sums = ns2[...]
    for i in range(len(dp_peers)):
        sums = sums + nr2[i]
    ratio = jnp.sqrt(sums[0:1] / (sums[1:2] + 1e-06))
    row_ratio = jnp.sum(member * ratio, axis=1, keepdims=True)
    step_size = learn_rate * row_ratio * gs[...]
    d[z, x, y] = (-step_size).astype(bf16)
    nm_ref[...] = ma_ref[...] - step_size

    p_cols = pl.ds(0, PA)
    q_cols = pl.ds(PA, PC)
    halves = (pl.ds(0, 512), pl.ds(512, PA - 512))

    def hop(ref, dev):
        return send(ref, ref, dev)

    cy = [hop(d.at[z, x, y, :, q_cols], dev) for dev in (yu, yd, y2)]
    az, ax, ayu, ayd, afw = {}, {}, {}, {}, []
    az[1] = [hop(d.at[z, x, y, :, p_cols], dev) for dev in (zu, zd)]

    def y_out(dz, other):
        h = ox if other else x
        ref = d.at[zo(dz), h, y, :, p_cols]
        ayu[dz, other] = hop(ref, yu)
        ayd[dz, other] = hop(ref, yd)

    def x_out(dz):
        ax[dz] = hop(d.at[zo(dz), x, y, :, p_cols], xp)

    def x_in(*dzs):
        for dz in dzs:
            ax[dz].wait_recv()
            y_out(dz, True)

    def y_relay(dz, other):
        if other:
            ayd[dz, other].wait_recv()
            afw.append(hop(d.at[zo(dz), ox, yo(1), :, p_cols], yd))
        else:
            ayu[dz, other].wait_recv()
            afw.append(hop(d.at[zo(dz), x, yo(-1), :, p_cols], yu))

    def z_in(step):
        for c in az[step]:
            c.wait_recv()
        if step < 3:
            az[step + 1] = [
                hop(d.at[zo(-step), x, y, :, p_cols], zu),
                hop(d.at[zo(step), x, y, :, p_cols], zd),
            ]
        elif step == 3:
            az[4] = [
                hop(d.at[zo(-3), x, y, :, halves[0]], zu),
                hop(d.at[zo(3), x, y, :, halves[1]], zd),
            ]
        for dz in (-step, step) if step < 4 else (4,):
            x_out(dz)
            y_out(dz, False)

    cz = {}

    def q_out(step, other):
        h = ox if other else x
        far = step - 1
        cz[step, other] = {}
        for s, dev in ((0, zu), (1, zd)):
            if step == 4 and s != int(other):
                continue
            cz[step, other][s] = hop(d.at[zo(-far if s == 0 else far), h, :, :, q_cols], dev)

    def q_in(step, other):
        for s, c in cz[step, other].items():
            c.wait_recv()
        if step < 4:
            q_out(step + 1, other)

    x_out(0)
    y_out(0, False)
    for c in cy:
        c.wait_recv()
    q_out(1, False)
    cx = hop(d.at[z, x, :, :, q_cols], xp)
    z_in(1)
    x_in(0)
    y_relay(0, False)
    q_in(1, False)
    cx.wait_recv()
    q_out(1, True)
    z_in(2)
    x_in(1, -1)
    y_relay(1, False)
    y_relay(-1, False)
    q_in(2, False)
    q_in(1, True)
    z_in(3)
    y_relay(0, True)
    x_in(2, -2)
    y_relay(2, False)
    y_relay(-2, False)
    q_in(3, False)
    q_in(2, True)
    z_in(4)
    y_relay(1, True)
    y_relay(-1, True)
    x_in(3, -3)
    y_relay(3, False)
    y_relay(-3, False)
    q_in(3, True)
    x_in(4)
    y_relay(2, True)
    y_relay(-2, True)
    y_relay(4, False)
    y_relay(3, True)
    y_relay(-3, True)
    y_relay(4, True)
    for key, c in ayd.items():
        if not key[1]:
            c.wait_recv()
    for key, c in ayu.items():
        if key[1]:
            c.wait_recv()
    q_in(4, False)
    q_in(4, True)
    for c in afw:
        c.wait_recv()

    def add(i, _):
        zz, h, v = lax.div(i, 8), lax.rem(lax.div(i, 4), 2), lax.rem(i, 4)
        nw_ref[i] = (w_ref[i].astype(f32) + d[zz, h, v].astype(f32)).astype(bf16)
        return 0

    lax.fori_loop(0, 64, add, 0)
    for c in sent:
        c.wait_send()


def on_device(gradients, weights, master, moment_one, moment_two, group_ids):
    vmem = pl.BlockSpec(memory_space=pltpu.VMEM)
    own = jax.ShapeDtypeStruct((ROWS, COLS), f32)
    V = pltpu.VMEM
    scratch = [
        V((NZ, NX, NY, ROWS, COLS), bf16),
        V((NZ, NX, NY, ROWS, COLS), bf16),
        V((8, 2, ROWS, CA), bf16),
        V((8, 2, ROWS, CA), bf16),
        V((8, 2, ROWS, CA), bf16),
        V((8, ROWS, CA), bf16),
        V((8, ROWS, CA), bf16),
        V((8, ROWS, CA), f32),
        V((8, ROWS, CA), f32),
        V((8, ROWS, CA), f32),
        V((8, ROWS, CA), f32),
        V((8, ROWS, CA), f32),
        V((2, NY, ROWS, CB), bf16),
        V((2, NY, ROWS, CB), bf16),
        V((2, 2, NY, ROWS, CB), bf16),
        V((2, 2, NY, ROWS, CB), f32),
        V((2, 2, NY, ROWS, CB), f32),
        V((2, 2, NY, ROWS, CB), f32),
        V((2, 2, NY, ROWS, CB), f32),
        V((2, NY, ROWS, CB), f32),
        V((2, ROWS, CB), f32),
        V((2, 2, ROWS, CB), f32),
        V((2, 2, ROWS, CB), f32),
        V((2, ROWS, CB), f32),
        V((ROWS, CB), f32),
        V((ROWS, COLS), f32),
        V((8, 128), f32),
        V((3, 8, 128), f32),
        V((8, 128), f32),
        V((8, 8, 128), f32),
        pltpu.SemaphoreType.DMA((8,)),
        pltpu.SemaphoreType.DMA((N_SEM,)),
        pltpu.SemaphoreType.DMA((N_SEM,)),
    ]
    new_weights, new_master, new_first, new_second = pl.pallas_call(
        kernel,
        out_shape=(jax.ShapeDtypeStruct((64, ROWS, COLS), bf16), own, own, own),
        in_specs=[pl.BlockSpec(memory_space=pl.ANY), vmem, vmem, vmem, vmem,
                  pl.BlockSpec(memory_space=pltpu.SMEM)],
        out_specs=(vmem, vmem, vmem, vmem),
        scratch_shapes=scratch,
        name="lamb",
        compiler_params=pltpu.CompilerParams(
            collective_id=0, has_side_effects=True, vmem_limit_bytes=48 * 2**20
        ),
    )(
        gradients.reshape(NZ, NX, NY, ROWS, COLS),
        weights.reshape(64, ROWS, COLS),
        master, moment_one, moment_two, group_ids,
    )
    return (new_weights.reshape(1024, COLS), new_master, new_first, new_second)


def solution(mesh):
    torus = Mesh(mesh.devices.reshape(8, 2, 4, 2, 2), NAMES)
    dp, mp = ("z", "xh", "y"), ("xl", "c")
    return jax.shard_map(
        on_device,
        mesh=torus,
        in_specs=(P(dp, None, mp), P(None, mp), P(dp, mp), P(dp, mp), P(dp, mp), P()),
        out_specs=(P(None, mp), P(dp, mp), P(dp, mp), P(dp, mp)),
        check_vma=False,
    )
```

time: 224 us -> 101 us (0.45)
  waiting for transfers between devices: 111 us -> 0 us
  Pallas kernels: 0 us -> 93 us
  blocking collectives: 71.1 us -> 0 us
  starting transfers between devices: 14.5 us -> 0 us
  between operations: 14.1 us -> 0.65 us
  other arithmetic: 7.49 us -> 0 us
  local copies, waits for them, and re-layouts: 2.71 us -> 6.94 us
    pallas_call x0 -> x1, Pallas kernels: none -> 93 us  [on_device(): pl.pallas_call(kernel, out_shape=(jax.ShapeDtypeStruct((64, ROWS, COLS),...]
    all_to_all x1 -> x0, waiting for transfers between devices: 72 us -> none  [summed_on_arrival(): lax.all_to_all(parts, axis, split_axis=0, concat_axis=0, tiled=True)]
    all_gather x1 -> x0, waiting for transfers between devices: 39.2 us -> none  [gather_in_order(): parts = lax.all_gather(parts, axes[k], axis=0, tiled=True)]
    psum x5 -> x0, blocking collectives: 36.8 us -> none  [by_axis(): return functools.reduce(lax.psum, axes, x)]
    all_gather x2 -> x0, blocking collectives: 34.3 us -> none  [gather_in_order(): parts = lax.all_gather(parts, axes[k], axis=0, tiled=True)]
    all_to_all x1 -> x0, starting transfers between devices: 14.5 us -> none  [summed_on_arrival(): lax.all_to_all(parts, axis, split_axis=0, concat_axis=0, tiled=True)]
    unnamed x8 -> x12, local copies, waits for them, and re-layouts: 1.45 us -> 6.94 us
    convert_element_type x2 -> x0, other arithmetic: 5.43 us -> none  [the longest x1 2.77 us: on_device(): whole_of(delta_bf, DP, (1, 0, 2), 0).astype(jnp.float32)]
  transfers between devices with their start and end apart: 2 -> 0, of which waited for: 2 -> 0; matrix products, arithmetic and copies ran while one was open for 0% -> 0% of each run, Pallas kernels for 0% -> 0%
where the time goes in v1:
time: 101 us
  Pallas kernels  93 us (92%)
  local copies, waits for them, and re-layouts  6.94 us (7%)
    pallas_call x1, Pallas kernels, on_device(): pl.pallas_call(kernel, out_shape=(jax.ShapeDtypeStruct((64, ROWS, COLS),...  93 us
    unnamed x12, local copies, waits for them, and re-layouts  6.94 us

profile of v1, /device:TPU:16, one launch (start us, length us, event | category | flops | bytes accessed | tf_op | source)
XLA Modules:
  0.0 100.6 jit_solution(9409606194118880551)
XLA Ops:
  0.6 0.0 copy-start
  0.6 0.9 copy-done
  1.5 0.0 copy-start.1
  1.5 0.9 copy-done.1
  2.4 0.0 copy-start.2
  2.4 0.9 copy-done.2
  3.3 0.0 copy-start.3
  3.3 0.7 copy-done.3
  4.0 93.0 %lamb.1 = (bf16[64,16,1536]{2,1,0:T(8,128)(2,1)S(1)}, f32[16,1536]{1,0:T(8,128)S(1)}, f32[16,1536]{1,0:T(8,128)S(1)}, f32[16,1536]{1,0:T(8,128)S(1)}) custom-call(bf16[8,2,4,16,1536]{4,3,2,1,0:T(8,128)(2,1)} %bitcast.4, bf16[64,16,1536]{2,1,0:T(8,128)(2,1)} %bitcast.5, f32[16,1536]{1,0:T(8,128)S(1)} %copy-done, f32[16,1536]{1,0:T(8,128)S(1)} %copy-done.1, ...), custom_call_target="tpu_custom_call" | custom-call | tf_op jit(solution)/shard_map/lamb/pallas_call | solution.py:459
  97.0 1.7 %copy.14 = bf16[1024,1536]{1,0:T(8,128)(2,1)} copy(bf16[1024,1536]{1,0:T(8,128)(2,1)S(1)} %bitcast.3) | data formatting | bytes 6291456
  98.6 0.6 copy.15
  99.3 0.6 copy.16
  99.9 0.6 copy.17
Async XLA Ops:
  0.6 0.9 copy-start
  1.5 0.9 copy-start.1
  2.4 0.9 copy-start.2
  3.3 0.7 copy-start.3

commit v2 on v0

v2 whole, which is shorter than its diff:
```python
import functools

import jax
import jax.numpy as jnp
from jax import lax
from jax.experimental import pallas as pl
from jax.experimental.pallas import tpu as pltpu
from jax.sharding import Mesh
from jax.sharding import PartitionSpec as P

MESH = pl.DeviceIdType.MESH
NAMES = ("z", "xh", "y", "xl", "c")
NZ, NX, NY = 8, 2, 4
ROWS, COLS = 16, 1536
CA = 1024
CB = COLS - CA
PA = 896
PC = COLS - PA
FAR = ((0, False), (4, True))
N_SEND, N_RECV = 21, 104

beta_one = 0.9
beta_two = 0.999
adam_eps = 1e-06
weight_decay = 0.01
learn_rate = 0.04
step_count = 100
correct_one = 1.0 - beta_one**step_count
correct_two = 1.0 - beta_two**step_count

f32, bf16 = jnp.float32, jnp.bfloat16


def kernel(
    g_hbm, w_hbm, in_ref, nw_ref, own_ref,
    g, d, w,
    ra, rl, xs, xr, yp, zs, zr,
    b4, bf4, b3, bs, br, bt, by2, bys, byr, bf, bxr,
    gs, norm_send, norm_recv, load_sem, send_sem, recv_sem,
):
    z, x, y = lax.axis_index("z"), lax.axis_index("xh"), lax.axis_index("y")
    xl, core = lax.axis_index("xl"), lax.axis_index("c")
    ox = 1 - x

    def zo(k):
        return lax.rem(z + (k + NZ), NZ)

    def yo(k):
        return lax.rem(y + (k + NY), NY)

    me = (z * NX + x) * NY + y

    def owner(k):
        o = lax.rem(me + (k + 64), 64)
        return {"z": lax.div(o, 8), "xh": lax.rem(lax.div(o, 4), 2), "y": lax.rem(o, 4)}

    yu, yd, y2 = {"y": yo(1)}, {"y": yo(-1)}, {"y": yo(2)}
    zu, zd, zu2, zd2 = ({"z": zo(k)} for k in (1, -1, 2, -2))
    xp = {"xh": ox}
    mp_far = ({}, {"c": 1 - core}, {"xl": 1 - xl}, {"xl": 1 - xl, "c": 1 - core})
    norm_peers = []
    for k in (4, -4, 3, -3, 2, -2, 1, -1, 0):
        to = owner(k) if k else {}
        norm_peers += [{**to, **far} for far in mp_far if k or far]

    barrier = pltpu.get_barrier_semaphore()
    cross_peers = [{**xp, **to} for to in (yu, yd, y2)]
    peers = [yu, yd, y2, zu, zd, zu2, zd2, xp] + cross_peers + norm_peers
    for p in peers:
        pl.semaphore_signal(barrier, 1, device_id=p, device_id_type=MESH)

    order = [4, 3, -3, 2, -2, 1, -1, 0]
    loads = []

    def load(src, dst):
        c = pltpu.make_async_copy(src, dst, load_sem.at[len(loads)])
        c.start()
        loads.append(c)

    for dz in order:
        load(g_hbm.at[zo(dz)], g.at[zo(dz)])
    load(w_hbm, w)

    pl.semaphore_wait(barrier, len(peers))

    send_ids, recv_ids = {}, {}

    def send(src, dst, dev, out, into):
        i = send_ids.setdefault(out, len(send_ids))
        j = recv_ids.setdefault(into, len(recv_ids))
        pltpu.make_async_remote_copy(
            src, dst, send_sem.at[i], recv_sem.at[j], device_id=dev, device_id_type=MESH
        ).start()

    def take(ref, sem):
        pltpu.make_async_copy(ref, ref, sem).wait()

    def arrived(ref, *into):
        take(ref, recv_sem.at[recv_ids[into]])

    def gone(ref, *out):
        take(ref, send_sem.at[send_ids[out]])

    a_cols = pl.ds(0, CA)
    b_cols = pl.ds(CA, CB)

    def y_start(k):
        zz = zo(order[k])
        send(g.at[zz, 0, yo(2), :, a_cols], rl.at[k, 0], yu, ("y",), ("rl", k))
        send(g.at[zz, 1, yo(2), :, a_cols], rl.at[k, 1], yd, ("y",), ("rl", k))

    def y_direct(k):
        zz = zo(order[k])
        send(g.at[zz, :, yo(1), :, a_cols], ra.at[k, pl.ds(0, 2)], yu, ("y",), ("ra", k))
        send(g.at[zz, :, yo(-1), :, a_cols], ra.at[k, pl.ds(2, 2)], yd, ("y",), ("ra", k))

    def y_forward(k):
        arrived(rl.at[k], "rl", k)
        send(rl.at[k, 0], ra.at[k, 4], yu, ("y",), ("ra", k))
        send(rl.at[k, 1], ra.at[k, 5], yd, ("y",), ("ra", k))

    def y_sum(k):
        arrived(ra.at[k], "ra", k)
        zz = zo(order[k])

        def total(h):
            return (
                (g[zz, h, y, :, 0:CA].astype(f32) + ra[k, h].astype(f32))
                + (ra[k, 2 + h].astype(f32) + ra[k, 4 + h].astype(f32))
            )

        xs[k] = total(ox)
        send(xs.at[k], xr.at[k], xp, ("x",), ("x", k))
        yp[k] = total(x)

    def z_step(k):
        dz = order[k]
        arrived(xr.at[k], "x", k)
        part = yp[k] + xr[k]
        if dz == 4:
            zs[k] = part
            up, down = pl.ds(0, 8), pl.ds(8, 8)
            send(zs.at[k, up], zr.at[k, up], zu, ("z",), ("z", 4))
            send(zs.at[k, down], zr.at[k, down], zd, ("z",), ("z", -4))
            return
        if dz == 0:
            up, down = order.index(1), order.index(-1)
            arrived(zr.at[up], "z", 1)
            arrived(zr.at[down], "z", -1)
            gs[:, 0:CA] = part + (zr[up] + zr[down])
            return
        step = abs(dz)
        if step == 3:
            rows = slice(0, 8) if dz > 0 else slice(8, 16)
            rest = slice(8, 16) if dz > 0 else slice(0, 8)
            arrived(zr.at[0, pl.ds(0, 8)], "z", 4 if dz > 0 else -4)
            zs[k, rows] = part[rows] + zr[0, rows]
            zs[k, rest] = part[rest]
        else:
            far = dz + 1 if dz > 0 else dz - 1
            arrived(zr.at[order.index(far)], "z", far)
            zs[k] = part + zr[order.index(far)]
        send(zs.at[k], zr.at[k], zu if dz > 0 else zd, ("z",), ("z", dz))

    zdir = (zu, zd)
    sign = (1, -1)

    def own_b(dz, h):
        return g[zo(dz), h, :, :, CA:COLS].astype(f32)

    def b_raw4():
        for s in (0, 1):
            send(g.at[zo(4), s, :, :, b_cols], b4.at[s], zdir[s], ("b",), ("b4",))

    def b_raw3():
        for first in (True, False):
            for s in (0, 1):
                h = (1 - s) if first else s
                src = g.at[zo(3 * sign[s]), h, :, :, b_cols]
                send(src, b3.at[s, h], zdir[s], ("b",), ("b3", first))

    def b_forward():
        arrived(b4, "b4")
        for s in (0, 1):
            send(b4.at[s], bf4.at[s], zdir[s], ("b",), ("bf",))

    def b_two(first):
        arrived(b3.at[0], "b3", first)
        if not first:
            arrived(bf4, "bf")
        for s in (0, 1):
            h = (1 - s) if first else s
            v = own_b(2 * sign[s], h) + b3[s, h].astype(f32)
            if not first:
                v = v + bf4[s].astype(f32)
            bs[0, s, h] = v
            send(bs.at[0, s, h], br.at[0, s, h], zdir[s], ("bs",), ("b2", first))

    def b_one(first):
        arrived(br.at[0, 0], "b2", first)
        for s in (0, 1):
            h = (1 - s) if first else s
            bs[1, s, h] = own_b(sign[s], h) + br[0, s, h]
            send(bs.at[1, s, h], br.at[1, s, h], zdir[s], ("bs",), ("b1",))

    def b_total():
        arrived(br.at[1], "b1")
        for h in (0, 1):
            bt[h] = own_b(0, h) + (br[1, 0, h] + br[1, 1, h])
        send(bt.at[0, yo(2)], by2.at[0], yu, ("by2",), ("by2",))
        send(bt.at[1, yo(2)], by2.at[1], yd, ("by2",), ("by2",))

    def b_y_one():
        arrived(by2, "by2")
        bys[0, 0] = bt[0, yo(1)] + by2[0]
        bys[0, 1] = bt[1, yo(1)]
        send(bys.at[0], byr.at[0], yu, ("by",), ("by",))
        bys[1, 0] = bt[0, yo(-1)]
        bys[1, 1] = bt[1, yo(-1)] + by2[1]
        send(bys.at[1], byr.at[1], yd, ("by",), ("by",))

    def b_y_sum():
        arrived(byr, "by")
        bf[1] = bt[ox, y] + (byr[0, ox] + byr[1, ox])
        send(bf.at[1], bxr, xp, ("bx",), ("bx",))
        bf[0] = bt[x, y] + (byr[0, x] + byr[1, x])

    def b_final():
        arrived(bxr, "bx")
        gs[:, CA:COLS] = bf[0] + bxr[...]

    loads[0].wait()
    y_start(0)
    b_raw4()
    loads[1].wait()
    y_start(1)
    y_direct(0)
    loads[2].wait()
    b_raw3()
    for k in range(8):
        if k + 2 < 8:
            for j in (3, 4) if k == 1 else (k + 3,) if 1 < k < 5 else ():
                loads[j].wait()
            y_start(k + 2)
        for j in ((k,) if k < 2 else (2, 3) if k == 2 else (k + 1,)):
            if j < 8:
                y_forward(j)
        if k + 1 < 8:
            y_direct(k + 1)
        if k == 0:
            b_forward()
        if k == 1:
            b_two(True)
        if k == 2:
            b_two(False)
        if k == 3:
            b_one(True)
        if k == 4:
            b_one(False)
        if k >= 1:
            y_sum(k - 1)
        if k >= 3:
            z_step(k - 3)
        if k == 5:
            b_total()
        if k == 6:
            b_y_one()
    b_y_sum()
    z_step(5)
    y_sum(7)
    z_step(6)
    b_final()
    z_step(7)

    lane = lax.broadcasted_iota(jnp.int32, (ROWS, 128), 1)
    wide = (ROWS, 1024)
    mine = lax.broadcasted_iota(jnp.int32, wide, 1) == (
        lax.broadcasted_iota(jnp.int32, wide, 0) + me * ROWS
    )
    ids = jnp.sum(jnp.where(mine, in_ref[3, 0:1, 0:1024], 0.0), axis=1, keepdims=True)
    member = (ids == lane.astype(f32)).astype(f32)
    master = in_ref[0]
    mean = gs[...] / 64.0
    new_first = beta_one * in_ref[1] + (1.0 - beta_one) * mean
    new_second = beta_two * in_ref[2] + (1.0 - beta_two) * mean * mean
    own_ref[1] = new_first
    own_ref[2] = new_second
    update = (
        new_first / correct_one / (jnp.sqrt(new_second / correct_two) + adam_eps)
        + weight_decay * master
    )
    gs[...] = update
    weight_rows = jnp.sum(master * master, axis=1, keepdims=True)
    update_rows = jnp.sum(update * update, axis=1, keepdims=True)
    weight_part = jnp.sum(member * weight_rows, axis=0, keepdims=True)
    update_part = jnp.sum(member * update_rows, axis=0, keepdims=True)
    first = lax.broadcasted_iota(jnp.int32, (8, 128), 0) == 0
    norm_send[...] = jnp.where(first, weight_part, update_part)
    for i, p in enumerate(norm_peers):
        send(norm_send, norm_recv.at[i], p, ("norm",), ("norm",))
    arrived(norm_recv, "norm")
    sums = norm_send[...] + jnp.sum(norm_recv[...], axis=0)
    ratio = jnp.sqrt(sums[0:1] / (sums[1:2] + 1e-06))
    row_ratio = jnp.sum(member * ratio, axis=1, keepdims=True)
    step_size = learn_rate * row_ratio * gs[...]
    d[z, x, y] = (-step_size).astype(bf16)

    p_cols = pl.ds(0, PA)
    q_cols = pl.ds(PA, PC)
    halves = (pl.ds(0, 512), pl.ds(512, PA - 512))
    p_units = {1: d.at[0, 0, 0, :, p_cols], 2: d.at[0, :, 0, :, p_cols], 4: d.at[0, 0, :, :, p_cols],
               8: d.at[0, :, :, :, p_cols], 16: d.at[pl.ds(0, 2), :, :, :, p_cols],
               32: d.at[pl.ds(0, 4), :, :, :, p_cols]}
    q_units = {1: d.at[0, 0, 0, :, q_cols], 2: d.at[0, :, 0, :, q_cols], 4: d.at[0, 0, :, :, q_cols],
               8: d.at[0, :, :, :, q_cols], 16: d.at[pl.ds(0, 2), :, :, :, q_cols],
               32: d.at[pl.ds(0, 4), :, :, :, q_cols]}
    spans = (32, 16, 8, 4, 2, 1)
    count = {"p": 0, "q": 0}

    def hop(kind, ref, dev, *into, whole=True):
        group = next(i for i in range(6) if count[kind] < sum(spans[: i + 1]))
        send(ref, ref, dev, (kind, group), into)
        count[kind] += whole

    def z_own():
        ref = d.at[z, x, y, :, p_cols]
        for step, up, down in ((1, zu, zd), (2, zu2, zd2)):
            hop("p", ref, up, "az", step)
            hop("p", ref, down, "az", step)

    def y_out(other, *dzs):
        h = ox if other else x
        for dz in dzs:
            ref = d.at[zo(dz), h, y, :, p_cols]
            far = (dz, other) in FAR
            relayed = ("relay", abs(dz), other)
            hop("p", ref, yu, *(("end", dz) if far or other else relayed))
            hop("p", ref, yd, *(("end", dz) if far or not other else relayed))
            if far:
                hop("p", ref, y2, "far", dz)

    def x_out(*dzs):
        for dz in dzs:
            hop("p", d.at[zo(dz), x, y, :, p_cols], xp, "ax", abs(dz))

    def x_in(*dzs):
        arrived(p_units[len(dzs)], "ax", abs(dzs[0]))
        y_out(True, *dzs)

    def y_relay(other, *dzs):
        arrived(p_units[len(dzs)], "relay", abs(dzs[0]), other)
        for dz in dzs:
            if other:
                hop("p", d.at[zo(dz), ox, yo(1), :, p_cols], yd, "end", dz)
            else:
                hop("p", d.at[zo(dz), x, yo(-1), :, p_cols], yu, "end", dz)

    def z_in(step):
        arrived(p_units[1 if step == 4 else 2], "az", step)
        if step == 2:
            hop("p", d.at[zo(-2), x, y, :, p_cols], zu, "az", 3)
            hop("p", d.at[zo(2), x, y, :, p_cols], zd, "az", 3)
            hop("p", d.at[zo(-2), x, y, :, halves[0]], zu2, "az", 4, whole=False)
            hop("p", d.at[zo(2), x, y, :, halves[1]], zd2, "az", 4)
        dzs = (-step, step) if step < 4 else (4,)
        x_out(*dzs)
        y_out(False, *dzs)

    def q_out(step, other, v):
        h = ox if other else x
        far = step - 1
        for s, dev in ((0, zu), (1, zd)):
            if step == 4 and s != int(other):
                continue
            if step == 4:
                into = ("q4",)
            elif step == 3 and s != int(other):
                into = ("q3", 3 if s else -3)
            else:
                into = ("q", step, other, v)
            hop("q", d.at[zo(-far if s == 0 else far), h, yo(v), :, q_cols], dev, *into)

    def q_in(step, other, *vs):
        for v in vs:
            arrived(q_units[1 if step == 3 else 2], "q", step, other, v)
            q_out(step + 1, other, v)

    def plane_out():
        ref = d.at[z, x, y, :, q_cols]
        for v, dev in ((-1, yu), (1, yd), (2, y2)):
            hop("q", ref, dev, "plane", False, v)
        hop("q", ref, xp, "plane", True, 0)
        for v, dev in zip((-1, 1, 2), cross_peers):
            hop("q", ref, dev, "plane", True, v)

    def plane_in(other, *vs):
        for v in vs:
            arrived(q_units[1], "plane", other, v)
            q_out(1, other, v)

    def slab_out(*dzs):
        for dz in dzs:
            arrived(p_units[4], "end", dz)
            if dz in (0, 4):
                arrived(p_units[1], "far", dz)
            if abs(dz) == 3:
                arrived(q_units[4], "q3", dz)
            if dz == 4:
                arrived(q_units[8], "q4")
            zz = zo(dz)

            def add(i, _):
                h, v = lax.div(i, NY), lax.rem(i, NY)
                nw_ref[zz, h, v] = (w[zz, h, v].astype(f32) + d[zz, h, v].astype(f32)).astype(bf16)
                return 0

            lax.fori_loop(0, NX * NY, add, 0)

    z_own()
    q_out(1, False, 0)
    plane_out()
    y_out(False, 0)
    x_out(0)
    own_ref[0] = in_ref[0] - step_size
    q_in(1, False, 0)
    z_in(1)
    plane_in(False, 1, -1)
    plane_in(True, 0)
    z_in(2)
    x_in(0)
    plane_in(False, 2)
    plane_in(True, 1, -1, 2)
    q_in(2, False, 0)
    y_relay(False, -1, 1)
    q_in(1, False, 1, -1)
    z_in(3)
    q_in(1, True, 0)
    x_in(-1, 1)
    q_in(1, False, 2)
    z_in(4)
    q_in(1, True, 1, -1, 2)
    y_relay(False, -2, 2)
    x_in(-2, 2)
    y_relay(True, 0)
    q_in(3, False, 0)
    q_in(2, False, 1, -1)
    q_in(2, True, 0)
    x_in(-3, 3)
    y_relay(False, -3, 3)
    q_in(2, False, 2)
    y_relay(True, -1, 1)
    x_in(4)
    q_in(2, True, 1, -1, 2)
    y_relay(True, -2, 2)
    y_relay(False, 4)
    q_in(3, False, 1, -1)
    q_in(3, True, 0)
    y_relay(True, -3, 3)
    q_in(3, False, 2)
    loads[8].wait()
    slab_out(0, -1, 1)
    q_in(3, True, 1, -1, 2)
    gone(g.at[:, :, :, :, a_cols], "y")
    gone(xs, "x")
    gone(zs.at[pl.ds(0, 7)], "z")
    gone(g.at[pl.ds(0, 4), :, :, :, b_cols], "b")
    gone(bs, "bs")
    gone(by2, "by2")
    gone(bys, "by")
    gone(bxr, "bx")
    gone(norm_recv, "norm")
    slab_out(-2, 2)
    slab_out(-3, 3)
    slab_out(4)
    for i, n in enumerate(spans):
        gone(p_units[n], "p", i)
        gone(q_units[n], "q", i)
    assert count == {"p": 63, "q": 63}
    assert (len(send_ids), len(recv_ids)) == (N_SEND, N_RECV), (len(send_ids), len(recv_ids))


def write_out(nw_ref, own_ref, nw_hbm, nm_hbm, nf_hbm, ns_hbm, sem):
    copies = []
    for i in range(4):
        rows = pl.ds(256 * i, 256)
        copies.append(pltpu.make_async_copy(nw_ref.at[rows], nw_hbm.at[rows], sem.at[i]))
    for i, to in enumerate((nm_hbm, nf_hbm, ns_hbm)):
        copies.append(pltpu.make_async_copy(own_ref.at[i], to, sem.at[4 + i]))
    for c in copies:
        c.start()
    for c in copies:
        c.wait()


def on_device(gradients, weights, master, moment_one, moment_two, group_ids):
    V = pltpu.VMEM
    scratch = [
        V((NZ, NX, NY, ROWS, COLS), bf16),
        V((NZ, NX, NY, ROWS, COLS), bf16),
        V((NZ, NX, NY, ROWS, COLS), bf16),
        V((8, 6, ROWS, CA), bf16),
        V((8, 2, ROWS, CA), bf16),
        V((8, ROWS, CA), f32),
        V((8, ROWS, CA), f32),
        V((8, ROWS, CA), f32),
        V((8, ROWS, CA), f32),
        V((8, ROWS, CA), f32),
        V((2, NY, ROWS, CB), bf16),
        V((2, NY, ROWS, CB), bf16),
        V((2, 2, NY, ROWS, CB), bf16),
        V((2, 2, 2, NY, ROWS, CB), f32),
        V((2, 2, 2, NY, ROWS, CB), f32),
        V((2, NY, ROWS, CB), f32),
        V((2, ROWS, CB), f32),
        V((2, 2, ROWS, CB), f32),
        V((2, 2, ROWS, CB), f32),
        V((2, ROWS, CB), f32),
        V((ROWS, CB), f32),
        V((ROWS, COLS), f32),
        V((8, 128), f32),
        V((35, 8, 128), f32),
        pltpu.SemaphoreType.DMA((9,)),
        pltpu.SemaphoreType.DMA((N_SEND,)),
        pltpu.SemaphoreType.DMA((N_RECV,)),
    ]
    hbm, vmem = pl.BlockSpec(memory_space=pltpu.HBM), pl.BlockSpec(memory_space=pltpu.VMEM)
    ids = jnp.pad(group_ids.astype(f32).reshape(1, 1024), ((0, ROWS - 1), (0, COLS - 1024)))
    inputs = jnp.stack([master, moment_one, moment_two, ids])
    new_weights, own = pl.pallas_call(
        kernel,
        out_shape=(
            jax.ShapeDtypeStruct((NZ, NX, NY, ROWS, COLS), bf16),
            jax.ShapeDtypeStruct((3, ROWS, COLS), f32),
        ),
        in_specs=[hbm, hbm, vmem],
        out_specs=(vmem, vmem),
        scratch_shapes=scratch,
        name="lamb",
        compiler_params=pltpu.CompilerParams(
            collective_id=0, has_side_effects=True, vmem_limit_bytes=48 * 2**20
        ),
    )(
        gradients.reshape(NZ, NX, NY, ROWS, COLS),
        weights.reshape(NZ, NX, NY, ROWS, COLS),
        inputs,
    )
    row_block = jax.ShapeDtypeStruct((ROWS, COLS), f32)
    new_weights, new_master, new_first, new_second = pl.pallas_call(
        write_out,
        out_shape=(jax.ShapeDtypeStruct((1024, COLS), bf16),) + (row_block,) * 3,
        in_specs=[pl.BlockSpec(memory_space=pl.ANY)] * 2,
        out_specs=(hbm,) * 4,
        scratch_shapes=[pltpu.SemaphoreType.DMA((7,))],
        compiler_params=pltpu.CompilerParams(vmem_limit_bytes=2**20),
        name="out",
    )(new_weights.reshape(1024, COLS), own)
    return (new_weights, new_master, new_first, new_second)


def solution(mesh):
    torus = Mesh(mesh.devices.reshape(8, 2, 4, 2, 2), NAMES)
    dp, mp = ("z", "xh", "y"), ("xl", "c")
    return jax.shard_map(
        on_device,
        mesh=torus,
        in_specs=(P(dp, None, mp), P(None, mp), P(dp, mp), P(dp, mp), P(dp, mp), P()),
        out_specs=(P(None, mp), P(dp, mp), P(dp, mp), P(dp, mp)),
        check_vma=False,
    )
```

time: 224 us -> 78.6 us (0.35)
  waiting for transfers between devices: 111 us -> 0 us
  Pallas kernels: 0 us -> 76.1 us
  blocking collectives: 71.1 us -> 0 us
  starting transfers between devices: 14.5 us -> 0 us
  between operations: 14.1 us -> 0.64 us
  other arithmetic: 7.49 us -> 1.71 us
  local copies, waits for them, and re-layouts: 2.71 us -> 0.01 us
    pallas_call x0 -> x2, Pallas kernels: none -> 76.1 us  [the longest x1 74.3 us: on_device(): pl.pallas_call(kernel, out_shape=(jax.ShapeDtypeStruct((NZ, NX, NY, ROWS,...]
    all_to_all x1 -> x0, waiting for transfers between devices: 72 us -> none  [summed_on_arrival(): lax.all_to_all(parts, axis, split_axis=0, concat_axis=0, tiled=True)]
    all_gather x1 -> x0, waiting for transfers between devices: 39.2 us -> none  [gather_in_order(): parts = lax.all_gather(parts, axes[k], axis=0, tiled=True)]
    psum x5 -> x0, blocking collectives: 36.8 us -> none  [by_axis(): return functools.reduce(lax.psum, axes, x)]
    all_gather x2 -> x0, blocking collectives: 34.3 us -> none  [gather_in_order(): parts = lax.all_gather(parts, axes[k], axis=0, tiled=True)]
    all_to_all x1 -> x0, starting transfers between devices: 14.5 us -> none  [summed_on_arrival(): lax.all_to_all(parts, axis, split_axis=0, concat_axis=0, tiled=True)]
    convert_element_type x2 -> x1, other arithmetic: 5.43 us -> 0.69 us  [on_device(): group_ids.astype(f32).reshape(1, 1024)]
  transfers between devices with their start and end apart: 2 -> 0, of which waited for: 2 -> 0; matrix products, arithmetic and copies ran while one was open for 0% -> 0% of each run, Pallas kernels for 0% -> 0%
where the time goes in v2:
time: 78.6 us; the launch traced here: 78.5 us
  Pallas kernels  76.1 us (97%)
  other arithmetic  1.71 us (2%)
    pallas_call x1, Pallas kernels, on_device(): pl.pallas_call(kernel, out_shape=(jax.ShapeDtypeStruct((NZ, NX, NY, ROWS,...  74.3 us
    pallas_call x1, Pallas kernels, on_device(): pl.pallas_call(write_out, out_shape=(jax.ShapeDtypeStruct((1024, COLS), b...  1.8 us

profile of v2, /device:TPU:16, one launch (start us, length us, event | category | flops | bytes accessed | tf_op | source)
XLA Modules:
  0.0 78.5 jit_solution(2231742909589088601)
XLA Ops:
  0.6 0.7 convert_element_type.5
  1.3 1.0 %pad_maximum_fusion.in_ref = f32[4,16,1536]{2,1,0:T(8,128)S(1)} fusion(f32[1,16,1536]{2,1,0:T(8,128)S(1)} %pad_bitcast_fusion, f32[1,16,1536]{2,1,0:T(8,128)} %bitcast.12, f32[1,16,1536]{2,1,0:T(8,128)} %bitcast.13, f32[1,16,1536]{2,1,0:T(8,128)} %bitcast.14), kind=kLoop, calls=%fused_computation | loop fusion | flops 294912 | bytes 786432 | tf_op jit(solution)/shard_map/stack | solution.py:528
  2.4 74.3 %lamb.1 = (bf16[8,2,4,16,1536]{4,3,2,1,0:T(8,128)(2,1)S(1)}, f32[3,16,1536]{2,1,0:T(8,128)S(1)}) custom-call(bf16[8,2,4,16,1536]{4,3,2,1,0:T(8,128)(2,1)} %bitcast.10, bf16[8,2,4,16,1536]{4,3,2,1,0:T(8,128)(2,1)} %bitcast.11, f32[4,16,1536]{2,1,0:T(8,128)S(1)} %pad_maximum_fusion.in_ref), custom_call_target="tpu_custom_call" | custom-call | tf_op jit(solution)/shard_map/lamb/pallas_call | solution.py:529
  76.7 1.8 %out.1 = (bf16[1024,1536]{1,0:T(8,128)(2,1)}, f32[16,1536]{1,0:T(8,128)}, f32[16,1536]{1,0:T(8,128)}, f32[16,1536]{1,0:T(8,128)}) custom-call(bf16[1024,1536]{1,0:T(8,128)(2,1)S(1)} %bitcast.9, f32[3,16,1536]{2,1,0:T(8,128)S(1)} %get-tuple-element.7.own_ref), custom_call_target="tpu_custom_call" | custom-call | tf_op jit(solution)/shard_map/out/pallas_call | solution.py:548
  (1 shorter events, 0.0 us)

commit v3 on v2

--- a/solution.py
+++ b/solution.py
@@ -65,7 +65,7 @@
 
     barrier = pltpu.get_barrier_semaphore()
     cross_peers = [{**xp, **to} for to in (yu, yd, y2)]
-    peers = [yu, yd, y2, zu, zd, zu2, zd2, xp] + cross_peers + norm_peers
+    peers = [yu, yd, zu, zd, xp] + norm_peers[-3:]
     for p in peers:
         pl.semaphore_signal(barrier, 1, device_id=p, device_id_type=MESH)
 

time: 78.6 us -> 76.2 us (0.969)
  Pallas kernels: 76.1 us -> 73.6 us
    pallas_call x1, Pallas kernels: 74.3 us -> 71.8 us  [on_device(): pl.pallas_call(kernel, out_shape=(jax.ShapeDtypeStruct((NZ, NX, NY, ROWS,...]
where the time goes in v3:
time: 76.2 us; the launch traced here: 75.9 us
  Pallas kernels  73.6 us (97%)
  other arithmetic  1.71 us (2%)
    pallas_call x1, Pallas kernels, on_device(): pl.pallas_call(kernel, out_shape=(jax.ShapeDtypeStruct((NZ, NX, NY, ROWS,...  71.8 us
    pallas_call x1, Pallas kernels, on_device(): pl.pallas_call(write_out, out_shape=(jax.ShapeDtypeStruct((1024, COLS), b...  1.8 us

profile of v3, /device:TPU:16, one launch (start us, length us, event | category | flops | bytes accessed | tf_op | source)
XLA Modules:
  0.0 75.9 jit_solution(5863387291630206065)
XLA Ops:
  0.6 0.7 convert_element_type.5
  1.3 1.0 %pad_maximum_fusion.in_ref = f32[4,16,1536]{2,1,0:T(8,128)S(1)} fusion(f32[1,16,1536]{2,1,0:T(8,128)S(1)} %pad_bitcast_fusion, f32[1,16,1536]{2,1,0:T(8,128)} %bitcast.12, f32[1,16,1536]{2,1,0:T(8,128)} %bitcast.13, f32[1,16,1536]{2,1,0:T(8,128)} %bitcast.14), kind=kLoop, calls=%fused_computation | loop fusion | flops 294912 | bytes 786432 | tf_op jit(solution)/shard_map/stack | solution.py:528
  2.4 71.8 %lamb.1 = (bf16[8,2,4,16,1536]{4,3,2,1,0:T(8,128)(2,1)S(1)}, f32[3,16,1536]{2,1,0:T(8,128)S(1)}) custom-call(bf16[8,2,4,16,1536]{4,3,2,1,0:T(8,128)(2,1)} %bitcast.10, bf16[8,2,4,16,1536]{4,3,2,1,0:T(8,128)(2,1)} %bitcast.11, f32[4,16,1536]{2,1,0:T(8,128)S(1)} %pad_maximum_fusion.in_ref), custom_call_target="tpu_custom_call" | custom-call | tf_op jit(solution)/shard_map/lamb/pallas_call | solution.py:529
  74.1 1.8 %out.1 = (bf16[1024,1536]{1,0:T(8,128)(2,1)}, f32[16,1536]{1,0:T(8,128)}, f32[16,1536]{1,0:T(8,128)}, f32[16,1536]{1,0:T(8,128)}) custom-call(bf16[1024,1536]{1,0:T(8,128)(2,1)S(1)} %bitcast.9, f32[3,16,1536]{2,1,0:T(8,128)S(1)} %get-tuple-element.7.own_ref), custom_call_target="tpu_custom_call" | custom-call | tf_op jit(solution)/shard_map/out/pallas_call | solution.py:548
  (1 shorter events, 0.0 us)

commit v4 on v3

--- a/solution.py
+++ b/solution.py
@@ -12,12 +12,13 @@
 NAMES = ("z", "xh", "y", "xl", "c")
 NZ, NX, NY = 8, 2, 4
 ROWS, COLS = 16, 1536
-CA = 1024
-CB = COLS - CA
+CA = 896
+CB = 384
+CC = COLS - CA - CB
 PA = 896
 PC = COLS - PA
 FAR = ((0, False), (4, True))
-N_SEND, N_RECV = 21, 104
+N_SEND, N_RECV = 24, 118
 
 beta_one = 0.9
 beta_two = 0.999
@@ -35,7 +36,8 @@
     g_hbm, w_hbm, in_ref, nw_ref, own_ref,
     g, d, w,
     ra, rl, xs, xr, yp, zs, zr,
-    b4, bf4, b3, bs, br, bt, by2, bys, byr, bf, bxr,
+    b4, bf4, b3, bs, br, bt, near_a, near_b, bf, bxr,
+    cx, cs, cr, ct, cn,
     gs, norm_send, norm_recv, load_sem, send_sem, recv_sem,
 ):
     z, x, y = lax.axis_index("z"), lax.axis_index("xh"), lax.axis_index("y")
@@ -65,7 +67,7 @@
 
     barrier = pltpu.get_barrier_semaphore()
     cross_peers = [{**xp, **to} for to in (yu, yd, y2)]
-    peers = [yu, yd, zu, zd, xp] + norm_peers[-3:]
+    peers = [yu, yd, zu, zd, xp] + cross_peers + norm_peers[-3:]
     for p in peers:
         pl.semaphore_signal(barrier, 1, device_id=p, device_id_type=MESH)
 
@@ -101,8 +103,13 @@
     def gone(ref, *out):
         take(ref, send_sem.at[send_ids[out]])
 
+    plane = [(False, v, dev) for v, dev in ((1, yu), (-1, yd), (2, y2))]
+    plane += [(True, 0, xp)]
+    plane += [(True, v, dev) for v, dev in zip((1, -1, 2), cross_peers)]
+
     a_cols = pl.ds(0, CA)
     b_cols = pl.ds(CA, CB)
+    c_cols = pl.ds(CA + CB, CC)
 
     def y_start(k):
         zz = zo(order[k])
@@ -133,40 +140,78 @@
         send(xs.at[k], xr.at[k], xp, ("x",), ("x", k))
         yp[k] = total(x)
 
-    def z_step(k):
+    def ring(k, part, out, into, tag):
         dz = order[k]
-        arrived(xr.at[k], "x", k)
-        part = yp[k] + xr[k]
+        n = out.shape[1] // 2
+        low, high = pl.ds(0, n), pl.ds(n, n)
         if dz == 4:
-            zs[k] = part
-            up, down = pl.ds(0, 8), pl.ds(8, 8)
-            send(zs.at[k, up], zr.at[k, up], zu, ("z",), ("z", 4))
-            send(zs.at[k, down], zr.at[k, down], zd, ("z",), ("z", -4))
-            return
+            out[k] = part
+            send(out.at[k, low], into.at[k, low], zu, (tag,), (tag, 4))
+            send(out.at[k, high], into.at[k, high], zd, (tag,), (tag, -4))
+            return None
         if dz == 0:
             up, down = order.index(1), order.index(-1)
-            arrived(zr.at[up], "z", 1)
-            arrived(zr.at[down], "z", -1)
-            gs[:, 0:CA] = part + (zr[up] + zr[down])
-            return
-        step = abs(dz)
-        if step == 3:
-            rows = slice(0, 8) if dz > 0 else slice(8, 16)
-            rest = slice(8, 16) if dz > 0 else slice(0, 8)
-            arrived(zr.at[0, pl.ds(0, 8)], "z", 4 if dz > 0 else -4)
-            zs[k, rows] = part[rows] + zr[0, rows]
-            zs[k, rest] = part[rest]
+            arrived(into.at[up], tag, 1)
+            arrived(into.at[down], tag, -1)
+            return part + (into[up] + into[down])
+        if abs(dz) == 3:
+            rows, rest = slice(0, n), slice(n, 2 * n)
+            if dz < 0:
+                rows, rest = rest, rows
+            arrived(into.at[0, low], tag, 4 if dz > 0 else -4)
+            out[k, rows] = part[rows] + into[0, rows]
+            out[k, rest] = part[rest]
         else:
             far = dz + 1 if dz > 0 else dz - 1
-            arrived(zr.at[order.index(far)], "z", far)
-            zs[k] = part + zr[order.index(far)]
-        send(zs.at[k], zr.at[k], zu if dz > 0 else zd, ("z",), ("z", dz))
+            arrived(into.at[order.index(far)], tag, far)
+            out[k] = part + into[order.index(far)]
+        send(out.at[k], into.at[k], zu if dz > 0 else zd, (tag,), (tag, dz))
+        return None
+
+    def z_step(k):
+        arrived(xr.at[k], "x", k)
+        ring(k, yp[k] + xr[k], zs, zr, "z")
+
+    def near_out(across):
+        for i, (other, v, dev) in enumerate(plane):
+            if other != across:
+                continue
+            src = g.at[z, ox if other else x, yo(v), :, a_cols]
+            send(src, near_a.at[i], dev, ("near_a",), ("near_a",))
+
+    def near_in():
+        arrived(near_a, "near_a")
+        part = g[z, x, y, :, 0:CA].astype(f32)
+        for i in range(len(plane)):
+            part = part + near_a[i].astype(f32)
+        gs[:, 0:CA] = ring(7, part, zs, zr, "z")
+
+    def c_raw(*ks):
+        for k in ks:
+            send(g.at[zo(order[k]), ox, :, :, c_cols], cx.at[k], xp, ("cx",), ("cx", k))
+
+    def c_part(k):
+        arrived(cx.at[k], "cx", k)
+        return g[zo(order[k]), x, :, :, CA + CB : COLS].astype(f32) + cx[k].astype(f32)
+
+    def c_step(*ks):
+        for k in ks:
+            ring(k, c_part(k), cs, cr, "cz")
+
+    def c_total():
+        ct[...] = ring(7, c_part(7), cs, cr, "cz")
+        for i, (_, v, dev) in enumerate(plane[:3]):
+            send(ct.at[yo(v)], cn.at[i], dev, ("cn",), ("cn",))
+
+    def c_final():
+        arrived(cn, "cn")
+        gs[:, CA + CB : COLS] = (ct[y] + cn[0]) + (cn[1] + cn[2])
 
     zdir = (zu, zd)
     sign = (1, -1)
 
     def own_b(dz, h):
-        return g[zo(dz), h, :, :, CA:COLS].astype(f32)
+        return g[zo(dz), h, :, :, CA : CA + CB].astype(f32)
 
     def b_raw4():
         for s in (0, 1):
@@ -207,46 +252,44 @@
         arrived(br.at[1], "b1")
         for h in (0, 1):
             bt[h] = own_b(0, h) + (br[1, 0, h] + br[1, 1, h])
-        send(bt.at[0, yo(2)], by2.at[0], yu, ("by2",), ("by2",))
-        send(bt.at[1, yo(2)], by2.at[1], yd, ("by2",), ("by2",))
-
-    def b_y_one():
-        arrived(by2, "by2")
-        bys[0, 0] = bt[0, yo(1)] + by2[0]
-        bys[0, 1] = bt[1, yo(1)]
-        send(bys.at[0], byr.at[0], yu, ("by",), ("by",))
-        bys[1, 0] = bt[0, yo(-1)]
-        bys[1, 1] = bt[1, yo(-1)] + by2[1]
-        send(bys.at[1], byr.at[1], yd, ("by",), ("by",))
+        for i, (_, v, dev) in enumerate(plane[:3]):
+            send(bt.at[:, yo(v)], near_b.at[i], dev, ("near_b",), ("near_b",))
 
     def b_y_sum():
-        arrived(byr, "by")
-        bf[1] = bt[ox, y] + (byr[0, ox] + byr[1, ox])
+        arrived(near_b, "near_b")
+        bf[1] = (bt[ox, y] + near_b[0, ox]) + (near_b[1, ox] + near_b[2, ox])
         send(bf.at[1], bxr, xp, ("bx",), ("bx",))
-        bf[0] = bt[x, y] + (byr[0, x] + byr[1, x])
+        bf[0] = (bt[x, y] + near_b[0, x]) + (near_b[1, x] + near_b[2, x])
 
     def b_final():
         arrived(bxr, "bx")
-        gs[:, CA:COLS] = bf[0] + bxr[...]
+        gs[:, CA : CA + CB] = bf[0] + bxr[...]
 
     loads[0].wait()
     y_start(0)
     b_raw4()
+    c_raw(0)
     loads[1].wait()
     y_start(1)
     y_direct(0)
     loads[2].wait()
     b_raw3()
+    c_raw(1, 2)
+    for j in range(3, 8):
+        loads[j].wait()
+    near_out(True)
+    c_raw(3, 4, 5, 6, 7)
+    y_start(2)
     for k in range(8):
-        if k + 2 < 8:
-            for j in (3, 4) if k == 1 else (k + 3,) if 1 < k < 5 else ():
-                loads[j].wait()
-            y_start(k + 2)
+        if k + 3 < 7:
+            y_start(k + 3)
         for j in ((k,) if k < 2 else (2, 3) if k == 2 else (k + 1,)):
-            if j < 8:
+            if j < 7:
                 y_forward(j)
-        if k + 1 < 8:
+        if k + 1 < 7:
             y_direct(k + 1)
+        if k == 6:
+            near_out(False)
         if k == 0:
             b_forward()
         if k == 1:
@@ -261,16 +304,23 @@
             y_sum(k - 1)
         if k >= 3:
             z_step(k - 3)
+        if k == 1:
+            c_step(0)
+        if k == 2:
+            c_step(1, 2)
+        if k == 4:
+            c_step(3, 4)
         if k == 5:
             b_total()
         if k == 6:
-            b_y_one()
+            c_step(5, 6)
     b_y_sum()
     z_step(5)
-    y_sum(7)
+    c_total()
     z_step(6)
     b_final()
-    z_step(7)
+    c_final()
+    near_in()
 
     lane = lax.broadcasted_iota(jnp.int32, (ROWS, 128), 1)
     wide = (ROWS, 1024)
@@ -386,12 +436,8 @@
             q_out(step + 1, other, v)
 
     def plane_out():
-        ref = d.at[z, x, y, :, q_cols]
-        for v, dev in ((-1, yu), (1, yd), (2, y2)):
-            hop("q", ref, dev, "plane", False, v)
-        hop("q", ref, xp, "plane", True, 0)
-        for v, dev in zip((-1, 1, 2), cross_peers):
-            hop("q", ref, dev, "plane", True, v)
+        for other, v, dev in plane:
+            hop("q", d.at[z, x, y, :, q_cols], dev, "plane", other, v if v == 2 else -v)
 
     def plane_in(other, *vs):
         for v in vs:
@@ -460,14 +506,17 @@
     loads[8].wait()
     slab_out(0, -1, 1)
     q_in(3, True, 1, -1, 2)
-    gone(g.at[:, :, :, :, a_cols], "y")
+    gone(g.at[pl.ds(0, 7), :, :, :, a_cols], "y")
     gone(xs, "x")
-    gone(zs.at[pl.ds(0, 7)], "z")
+    gone(zs, "z")
     gone(g.at[pl.ds(0, 4), :, :, :, b_cols], "b")
     gone(bs, "bs")
-    gone(by2, "by2")
-    gone(bys, "by")
+    gone(near_a, "near_a")
+    gone(near_b, "near_b")
     gone(bxr, "bx")
+    gone(cx, "cx")
+    gone(cs, "cz")
+    gone(cn, "cn")
     gone(norm_recv, "norm")
     slab_out(-2, 2)
     slab_out(-3, 3)
@@ -498,24 +547,28 @@
         V((NZ, NX, NY, ROWS, COLS), bf16),
         V((NZ, NX, NY, ROWS, COLS), bf16),
         V((NZ, NX, NY, ROWS, COLS), bf16),
-        V((8, 6, ROWS, CA), bf16),
-        V((8, 2, ROWS, CA), bf16),
-        V((8, ROWS, CA), f32),
-        V((8, ROWS, CA), f32),
-        V((8, ROWS, CA), f32),
-        V((8, ROWS, CA), f32),
-        V((8, ROWS, CA), f32),
+        V((7, 6, ROWS, CA), bf16),
+        V((7, 2, ROWS, CA), bf16),
+        V((7, ROWS, CA), f32),
+        V((7, ROWS, CA), f32),
+        V((7, ROWS, CA), f32),
+        V((7, ROWS, CA), f32),
+        V((7, ROWS, CA), f32),
         V((2, NY, ROWS, CB), bf16),
         V((2, NY, ROWS, CB), bf16),
         V((2, 2, NY, ROWS, CB), bf16),
         V((2, 2, 2, NY, ROWS, CB), f32),
         V((2, 2, 2, NY, ROWS, CB), f32),
         V((2, NY, ROWS, CB), f32),
-        V((2, ROWS, CB), f32),
-        V((2, 2, ROWS, CB), f32),
-        V((2, 2, ROWS, CB), f32),
+        V((7, ROWS, CA), bf16),
+        V((3, 2, ROWS, CB), f32),
         V((2, ROWS, CB), f32),
         V((ROWS, CB), f32),
+        V((8, NY, ROWS, CC), bf16),
+        V((7, NY, ROWS, CC), f32),
+        V((7, NY, ROWS, CC), f32),
+        V((NY, ROWS, CC), f32),
+        V((3, ROWS, CC), f32),
         V((ROWS, COLS), f32),
         V((8, 128), f32),
         V((35, 8, 128), f32),

time: 76.2 us -> 76.3 us (level)
  no operation moved by 1% of the time
where the time goes in v4:
time: 76.3 us; the launch traced here: 76.2 us
  Pallas kernels  73.8 us (97%)
  other arithmetic  1.71 us (2%)
    pallas_call x1, Pallas kernels, on_device(): pl.pallas_call(kernel, out_shape=(jax.ShapeDtypeStruct((NZ, NX, NY, ROWS,...  72 us
    pallas_call x1, Pallas kernels, on_device(): pl.pallas_call(write_out, out_shape=(jax.ShapeDtypeStruct((1024, COLS), b...  1.8 us

profile of v4, /device:TPU:16, one launch (start us, length us, event | category | flops | bytes accessed | tf_op | source)
XLA Modules:
  0.0 76.2 jit_solution(8417405698158586547)
XLA Ops:
  0.6 0.7 convert_element_type.5
  1.3 1.0 %pad_maximum_fusion.in_ref = f32[4,16,1536]{2,1,0:T(8,128)S(1)} fusion(f32[1,16,1536]{2,1,0:T(8,128)S(1)} %pad_bitcast_fusion, f32[1,16,1536]{2,1,0:T(8,128)} %bitcast.12, f32[1,16,1536]{2,1,0:T(8,128)} %bitcast.13, f32[1,16,1536]{2,1,0:T(8,128)} %bitcast.14), kind=kLoop, calls=%fused_computation | loop fusion | flops 294912 | bytes 786432 | tf_op jit(solution)/shard_map/stack | solution.py:581
  2.4 72.0 %lamb.1 = (bf16[8,2,4,16,1536]{4,3,2,1,0:T(8,128)(2,1)S(1)}, f32[3,16,1536]{2,1,0:T(8,128)S(1)}) custom-call(bf16[8,2,4,16,1536]{4,3,2,1,0:T(8,128)(2,1)} %bitcast.10, bf16[8,2,4,16,1536]{4,3,2,1,0:T(8,128)(2,1)} %bitcast.11, f32[4,16,1536]{2,1,0:T(8,128)S(1)} %pad_maximum_fusion.in_ref), custom_call_target="tpu_custom_call" | custom-call | tf_op jit(solution)/shard_map/lamb/pallas_call | solution.py:582
  74.4 1.8 %out.1 = (bf16[1024,1536]{1,0:T(8,128)(2,1)}, f32[16,1536]{1,0:T(8,128)}, f32[16,1536]{1,0:T(8,128)}, f32[16,1536]{1,0:T(8,128)}) custom-call(bf16[1024,1536]{1,0:T(8,128)(2,1)S(1)} %bitcast.9, f32[3,16,1536]{2,1,0:T(8,128)S(1)} %get-tuple-element.7.own_ref), custom_call_target="tpu_custom_call" | custom-call | tf_op jit(solution)/shard_map/out/pallas_call | solution.py:601
  (1 shorter events, 0.0 us)

commit v5 on v4

--- a/solution.py
+++ b/solution.py
@@ -67,7 +67,7 @@
 
     barrier = pltpu.get_barrier_semaphore()
     cross_peers = [{**xp, **to} for to in (yu, yd, y2)]
-    peers = [yu, yd, zu, zd, xp] + cross_peers + norm_peers[-3:]
+    peers = [yu, yd, zu, zd, xp] + norm_peers[-3:]
     for p in peers:
         pl.semaphore_signal(barrier, 1, device_id=p, device_id_type=MESH)
 
@@ -277,7 +277,6 @@
     c_raw(1, 2)
     for j in range(3, 8):
         loads[j].wait()
-    near_out(True)
     c_raw(3, 4, 5, 6, 7)
     y_start(2)
     for k in range(8):
@@ -305,6 +304,7 @@
         if k >= 3:
             z_step(k - 3)
         if k == 1:
+            near_out(True)
             c_step(0)
         if k == 2:
             c_step(1, 2)

time: 76.3 us -> 73.8 us (0.967)
  Pallas kernels: 73.8 us -> 71.3 us
    pallas_call x1, Pallas kernels: 72 us -> 69.5 us  [on_device(): pl.pallas_call(kernel, out_shape=(jax.ShapeDtypeStruct((NZ, NX, NY, ROWS,...]
where the time goes in v5:
time: 73.8 us; the launch traced here: 73.6 us
  Pallas kernels  71.3 us (97%)
  other arithmetic  1.71 us (2%)
    pallas_call x1, Pallas kernels, on_device(): pl.pallas_call(kernel, out_shape=(jax.ShapeDtypeStruct((NZ, NX, NY, ROWS,...  69.5 us
    pallas_call x1, Pallas kernels, on_device(): pl.pallas_call(write_out, out_shape=(jax.ShapeDtypeStruct((1024, COLS), b...  1.8 us

profile of v5, /device:TPU:16, one launch (start us, length us, event | category | flops | bytes accessed | tf_op | source)
XLA Modules:
  0.0 73.6 jit_solution(13233101680134877453)
XLA Ops:
  0.6 0.7 convert_element_type.5
  1.3 1.0 %pad_maximum_fusion.in_ref = f32[4,16,1536]{2,1,0:T(8,128)S(1)} fusion(f32[1,16,1536]{2,1,0:T(8,128)S(1)} %pad_bitcast_fusion, f32[1,16,1536]{2,1,0:T(8,128)} %bitcast.12, f32[1,16,1536]{2,1,0:T(8,128)} %bitcast.13, f32[1,16,1536]{2,1,0:T(8,128)} %bitcast.14), kind=kLoop, calls=%fused_computation | loop fusion | flops 294912 | bytes 786432 | tf_op jit(solution)/shard_map/stack | solution.py:581
  2.4 69.5 %lamb.1 = (bf16[8,2,4,16,1536]{4,3,2,1,0:T(8,128)(2,1)S(1)}, f32[3,16,1536]{2,1,0:T(8,128)S(1)}) custom-call(bf16[8,2,4,16,1536]{4,3,2,1,0:T(8,128)(2,1)} %bitcast.10, bf16[8,2,4,16,1536]{4,3,2,1,0:T(8,128)(2,1)} %bitcast.11, f32[4,16,1536]{2,1,0:T(8,128)S(1)} %pad_maximum_fusion.in_ref), custom_call_target="tpu_custom_call" | custom-call | tf_op jit(solution)/shard_map/lamb/pallas_call | solution.py:582
  71.8 1.8 %out.1 = (bf16[1024,1536]{1,0:T(8,128)(2,1)}, f32[16,1536]{1,0:T(8,128)}, f32[16,1536]{1,0:T(8,128)}, f32[16,1536]{1,0:T(8,128)}) custom-call(bf16[1024,1536]{1,0:T(8,128)(2,1)S(1)} %bitcast.9, f32[3,16,1536]{2,1,0:T(8,128)S(1)} %get-tuple-element.7.own_ref), custom_call_target="tpu_custom_call" | custom-call | tf_op jit(solution)/shard_map/out/pallas_call | solution.py:601
  (1 shorter events, 0.0 us)

commit v6 on v5

--- a/solution.py
+++ b/solution.py
@@ -462,9 +462,9 @@
 
             lax.fori_loop(0, NX * NY, add, 0)
 
-    z_own()
     q_out(1, False, 0)
     plane_out()
+    z_own()
     y_out(False, 0)
     x_out(0)
     own_ref[0] = in_ref[0] - step_size

time: 73.8 us -> 73 us (0.989)
  Pallas kernels: 71.3 us -> 70.5 us
    pallas_call x1, Pallas kernels: 69.5 us -> 68.7 us  [on_device(): pl.pallas_call(kernel, out_shape=(jax.ShapeDtypeStruct((NZ, NX, NY, ROWS,...]
where the time goes in v6:
time: 73 us; the launch traced here: 72.9 us
  Pallas kernels  70.5 us (97%)
  other arithmetic  1.71 us (2%)
    pallas_call x1, Pallas kernels, on_device(): pl.pallas_call(kernel, out_shape=(jax.ShapeDtypeStruct((NZ, NX, NY, ROWS,...  68.7 us
    pallas_call x1, Pallas kernels, on_device(): pl.pallas_call(write_out, out_shape=(jax.ShapeDtypeStruct((1024, COLS), b...  1.8 us

profile of v6, /device:TPU:16, one launch (start us, length us, event | category | flops | bytes accessed | tf_op | source)
XLA Modules:
  0.0 72.9 jit_solution(12347668100708208287)
XLA Ops:
  0.6 0.7 convert_element_type.5
  1.3 1.0 %pad_maximum_fusion.in_ref = f32[4,16,1536]{2,1,0:T(8,128)S(1)} fusion(f32[1,16,1536]{2,1,0:T(8,128)S(1)} %pad_bitcast_fusion, f32[1,16,1536]{2,1,0:T(8,128)} %bitcast.12, f32[1,16,1536]{2,1,0:T(8,128)} %bitcast.13, f32[1,16,1536]{2,1,0:T(8,128)} %bitcast.14), kind=kLoop, calls=%fused_computation | loop fusion | flops 294912 | bytes 786432 | tf_op jit(solution)/shard_map/stack | solution.py:581
  2.4 68.7 %lamb.1 = (bf16[8,2,4,16,1536]{4,3,2,1,0:T(8,128)(2,1)S(1)}, f32[3,16,1536]{2,1,0:T(8,128)S(1)}) custom-call(bf16[8,2,4,16,1536]{4,3,2,1,0:T(8,128)(2,1)} %bitcast.10, bf16[8,2,4,16,1536]{4,3,2,1,0:T(8,128)(2,1)} %bitcast.11, f32[4,16,1536]{2,1,0:T(8,128)S(1)} %pad_maximum_fusion.in_ref), custom_call_target="tpu_custom_call" | custom-call | tf_op jit(solution)/shard_map/lamb/pallas_call | solution.py:582
  71.1 1.8 %out.1 = (bf16[1024,1536]{1,0:T(8,128)(2,1)}, f32[16,1536]{1,0:T(8,128)}, f32[16,1536]{1,0:T(8,128)}, f32[16,1536]{1,0:T(8,128)}) custom-call(bf16[1024,1536]{1,0:T(8,128)(2,1)S(1)} %bitcast.9, f32[3,16,1536]{2,1,0:T(8,128)S(1)} %get-tuple-element.7.own_ref), custom_call_target="tpu_custom_call" | custom-call | tf_op jit(solution)/shard_map/out/pallas_call | solution.py:601
  (1 shorter events, 0.0 us)
